TPU v7x, 32 devices: a whole 2x2x4 slice. The times are simulated.
32 devices in a mesh: role: 2 (over x), dp: 4 (over y, core), ctx: 4 (over z).
Axes of the slice: x: 2, y: 2, z: 4, core: 2. Of those that a mesh axis runs over, the one named last changes fastest.
Arguments:
- teacher_states: bfloat16 [4, 512, 5120], P('dp', 'ctx'), may hold values from -50 to 50
- student_states: bfloat16 [4, 512, 3584], P('dp', 'ctx'), may hold values from -50 to 50
- teacher_gain: float32 [5120], replicated, may hold values from 0.25 to 1.75
- student_gain: float32 [3584], replicated, may hold values from 0.25 to 1.75
- mentor_output_weights: bfloat16 [4, 5120, 2048], P(None, None, 'ctx'), may hold values from -2 to 2
- student_heads: bfloat16 [4, 3584, 2048], P(None, None, 'ctx'), may hold values from -2 to 2
- segments: int32 [4, 512], P('dp', 'ctx'), may hold values from 0 to 7, never falling along the last dimension, each value on 1 to 256 neighbouring positions
- targets: int32 [4, 512, 4], P('dp', 'ctx'), may hold values from 0 to 2047
Outputs:
- grad_heads: float32 [4, 3584, 2048], P(None, ('role', 'dp'), 'ctx')
- frame_terms: float32 [2, 4, 512, 4], P('role', 'dp', 'ctx')
All inputs are finite; a program needn't handle non-finite values.
Results may differ from a plain program's by a relative error of at most 0.0048.
Values may be sent and summed in bfloat16 or wider, within the bound.
A program may use at most 192 MiB of HBM per device.

v0:
```python
import functools
import itertools

import jax
import jax.numpy as jnp
from jax import lax
from jax.experimental import pallas as pl
from jax.experimental.pallas import tpu as pltpu
from jax.sharding import PartitionSpec as P

epsilon = 1e-06
sharpness_divisor = 2.0
blend_ratio = 0.5
sub = 16
lanes = 128
pitch = 8

MESH = pl.DeviceIdType.MESH
f32 = jnp.float32
bf16 = jnp.bfloat16


def normalize_rows(source, gain, target, width):
    step = 512 if width % 512 == 0 else 128
    total = jnp.zeros((sub, step), f32)
    for start in range(0, width, step):
        x = source[:, start : start + step].astype(f32)
        total = total + x * x
    factor = lax.rsqrt(jnp.sum(total, axis=1, keepdims=True) / width + epsilon)
    for start in range(0, width, step):
        x = source[:, start : start + step].astype(f32)
        target[:, start : start + step] = (x * factor * gain[:, start : start + step]).astype(bf16)


def kernel(
    sizes,
    teacher_in,
    student_in,
    teacher_gain,
    student_gain,
    teacher_weights_in,
    student_weights_in,
    packed_in,
    out,
    terms_out,
    teacher_raw,
    student_raw,
    teacher_weights,
    student_weights,
    teacher_normed,
    student_normed,
    slabs,
    features_all,
    slopes_all,
    scaled,
    logits,
    packed,
    target_lanes,
    weight_lanes,
    stat_rows,
    stats,
    norm_rows,
    gaps,
    gaps_in,
    own_terms,
    swap,
    z_send,
    z_recv,
    z_local,
    weights_sem,
    packed_send,
    packed_recv,
    stats_send,
    stats_recv,
    feature_send,
    feature_recv,
    slope_send,
    slope_recv,
    gap_send,
    gap_recv,
    swap_sem,
):
    roles, dps, planes, inner, books, columns, share, half = sizes
    outer = dps // inner
    places = roles * dps
    rounds = half // sub
    group = planes * sub
    role = lax.axis_index("role")
    dp = lax.axis_index("dp")
    plane = lax.axis_index("ctx")
    ring, core = dp // inner, dp % inner
    me = role * dps + dp
    widths = (teacher_in.shape[1], student_in.shape[1])
    inputs = (teacher_in, student_in)
    raws = (teacher_raw, student_raw)
    middle = jnp.logical_and(plane > 0, plane < planes - 1)

    shifts = [s for s in itertools.product(range(roles), range(outer), range(inner))]

    def peer(shift, sign=1):
        dr, do, di = shift
        r = lax.rem(role + sign * dr + roles, roles)
        o = lax.rem(ring + sign * do + outer, outer)
        i = lax.rem(core + sign * di + inner, inner)
        return r, o * inner + i

    def place_of(where):
        return where[0] * dps + where[1]

    def rows(index, size):
        return pl.ds(pl.multiple_of(index * size, size), size)

    def remote(src, dst, send, recv, device):
        return pltpu.make_async_remote_copy(
            src_ref=src, dst_ref=dst, send_sem=send, recv_sem=recv, device_id=device, device_id_type=MESH
        )

    def z_copy(kind, s, b, up, own):
        src = inputs[kind].at[rows(role * rounds + s, sub)] if own else raws[kind].at[s, b]
        target = plane + 1 if up else plane - 1
        return remote(
            src, raws[kind].at[s, b], z_send.at[int(up), kind, s, b], z_recv.at[kind, s, b], (role, dp, target)
        )

    def send_own(kind, s):
        @pl.when(plane < planes - 1)
        def _():
            z_copy(kind, s, plane, True, True).start()

        @pl.when(plane > 0)
        def _():
            z_copy(kind, s, plane, False, True).start()

    def z_arrive(kind, s, b):
        z_copy(kind, s, b, True, False).wait_recv()

    def pass_on(kind, s, hop):
        @pl.when(jnp.logical_and(middle, plane - hop >= 0))
        def _():
            b = plane - hop
            z_arrive(kind, s, b)
            z_copy(kind, s, b, True, False).start()

        @pl.when(jnp.logical_and(middle, plane + hop <= planes - 1))
        def _():
            b = plane + hop
            z_arrive(kind, s, b)
            z_copy(kind, s, b, False, False).start()

    def forward(s):
        for kind in range(2):
            pass_on(kind, s, 1)

            @pl.when(s + 2 < rounds)
            def _():
                send_own(kind, s + 2)

            def hops(h, carry):
                pass_on(kind, s, h)
                return carry

            if planes > 2:
                lax.fori_loop(2, planes, hops, 0)

    def own_local(kind, s):
        return pltpu.make_async_copy(
            inputs[kind].at[rows(role * rounds + s, sub)], raws[kind].at[s, plane], z_local.at[kind, s]
        )

    def weight_copy(kind, q):
        src, dst = ((teacher_weights_in, teacher_weights), (student_weights_in, student_weights))[kind]
        return pltpu.make_async_copy(src.at[q], dst.at[q], weights_sem.at[kind, q])

    def packed_copy(step, arriving):
        other = lax.rem(plane + (planes - step if arriving else step), planes)
        slot = other if arriving else plane
        return remote(
            packed.at[slot] if arriving else packed_in,
            packed.at[slot],
            packed_send.at[step],
            packed_recv.at[slot],
            (role, dp, other),
        )

    def stats_copy(s, step, arriving):
        other = lax.rem(plane + (planes - step if arriving else step), planes)
        slot = other if arriving else plane
        return remote(
            stats.at[s, slot], stats.at[s, slot], stats_send.at[s, step], stats_recv.at[s, slot], (role, dp, other)
        )

    def gap_copy(step, arriving):
        other = lax.rem(plane + (planes - step if arriving else step), planes)
        slot = other if arriving else plane
        return remote(
            gaps.at[other], gaps_in.at[slot], gap_send.at[step], gap_recv.at[slot], (role, dp, other)
        )

    def feature_copy(s, n, arriving):
        where = peer(shifts[n], -1 if arriving else 1)
        there = place_of(where)
        slot = there if arriving else me
        return remote(
            slabs.at[s, there],
            features_all.at[s, rows(slot, group)],
            feature_send.at[s, n],
            feature_recv.at[s, slot],
            (where[0], where[1], plane),
        )

    def slope_copy(s, source, index, where):
        part = slopes_all.at[s, rows(source, group)]
        return remote(part, part, slope_send.at[s, index], slope_recv.at[s, source], (where[0], where[1], plane))

    faces = [(dr, do, 0) for dr, do in itertools.product(range(roles), range(outer)) if dr or do]
    cores = [(0, 0, di) for di in range(1, inner)]

    def over(count, body):
        def step(i, carry):
            body(i)
            return carry

        lax.fori_loop(0, count, step, 0)

    def project(kind, s, q):
        @pl.when(s == 0)
        def _():
            weight_copy(kind, q).wait()

        if kind == 0:
            scaled[q] = (
                jnp.dot(teacher_normed[...], teacher_weights[q], preferred_element_type=f32) / sharpness_divisor
            )
        else:
            logits[q] = jnp.dot(student_normed[...], student_weights[q], preferred_element_type=f32)

    def take(kind, s, b):
        @pl.when(b == plane)
        def _():
            own_local(kind, s).wait()

        @pl.when(jnp.logical_and(b != plane, jnp.logical_not(middle)))
        def _():
            z_arrive(kind, s, b)

        gain = (teacher_gain, student_gain)[kind]
        target = (teacher_normed, student_normed)[kind]
        normalize_rows(raws[kind].at[s, b], gain, target.at[rows(b, sub)], widths[kind])

    lane_of = lambda count: lax.broadcasted_iota(jnp.int32, (count, lanes), 1)

    def compute_logits(s):
        over(planes, lambda b: take(0, s, b))
        over(books, lambda q: project(0, s, q))
        over(planes, lambda b: take(1, s, b))

        def cut(b):
            for p in range(places):
                slabs[s, p, rows(b, sub), :] = student_normed[rows(b, sub), p * share : (p + 1) * share]

        over(planes, cut)
        features_all[s, rows(me, group), :] = slabs[s, me]
        over(books, lambda q: project(1, s, q))
        for n in range(1, places):
            feature_copy(s, n, False).start()

        positions = lax.broadcasted_iota(jnp.int32, (sub, columns), 1)
        lane = lane_of(sub)

        def totals(b):
            here = rows(b, sub)
            first = jnp.zeros((sub, lanes), f32)
            second = jnp.zeros((sub, lanes), f32)
            for q in range(books):
                hit = positions == target_lanes[s, here, q : q + 1]

                def put(array, kind, value):
                    return jnp.where(lane == kind * pitch + q, value, array)

                z = scaled[q, here, :]
                peak = jnp.max(z, axis=1, keepdims=True)
                first = put(first, 0, peak)
                first = put(first, 1, jnp.sum(jnp.exp(z - peak), axis=1, keepdims=True))
                first = put(first, 2, jnp.sum(jnp.where(hit, z, 0.0), axis=1, keepdims=True))
                u = logits[q, here, :]
                peak = jnp.max(u, axis=1, keepdims=True)
                centered = u - peak
                second = put(second, 0, peak)
                second = put(second, 1, jnp.sum(jnp.exp(centered), axis=1, keepdims=True))
                second = put(
                    second, 2, jnp.sum(jnp.exp(centered / sharpness_divisor), axis=1, keepdims=True)
                )
                second = put(second, 3, jnp.sum(jnp.where(hit, u, 0.0), axis=1, keepdims=True))
            stat_rows[here, :] = first
            stat_rows[rows(planes + b, sub), :] = second

        over(planes, totals)
        stats[s, plane] = jnp.transpose(stat_rows[...])[: 4 * pitch]

        def share_stats(step, carry):
            stats_copy(s, step, False).start()
            return carry

        lax.fori_loop(1, planes, share_stats, 0)

    def compute_slopes(s):
        def arrive(step, carry):
            stats_copy(s, step, True).wait_recv()
            return carry

        lax.fori_loop(1, planes, arrive, 0)

        def part(p, kind):
            return stats[s, p, kind * pitch : (kind + 1) * pitch, :]

        largest = lax.fori_loop(1, planes, lambda p, m: jnp.maximum(m, part(p, 0)), part(0, 0))

        def merge(p, carry):
            plain, warm, teacher_pick, student_pick = carry
            below = part(p, 0) - largest
            return (
                plain + part(p, 1) * jnp.exp(below),
                warm + part(p, 2) * jnp.exp(below / sharpness_divisor),
                teacher_pick + part(p, 2),
                student_pick + part(p, 3),
            )

        zero = jnp.zeros((pitch, 2 * group), f32)
        plain, warm, teacher_pick, student_pick = lax.fori_loop(0, planes, merge, (zero,) * 4)
        is_teacher = lax.broadcasted_iota(jnp.int32, (pitch, 2 * group), 1) < group
        plain_norm = largest + jnp.log(plain)
        warm_norm = largest / sharpness_divisor + jnp.log(jnp.where(is_teacher, 1.0, warm))
        term = plain_norm - jnp.where(is_teacher, teacher_pick, student_pick)
        merged = jnp.concatenate(
            [plain_norm, warm_norm, term, jnp.zeros((lanes - 3 * pitch, 2 * group), f32)], axis=0
        )
        norm_rows[...] = jnp.transpose(merged)
        own_terms[0, rows(s, sub), :] = norm_rows[rows(plane, sub), :]
        own_terms[1, rows(s, sub), :] = norm_rows[rows(planes + plane, sub), :]

        positions = lax.broadcasted_iota(jnp.int32, (sub, columns), 1)
        lane = lane_of(sub)

        def slope_rows(b):
            here = rows(b, sub)
            teacher_side = norm_rows[here, :]
            student_side = norm_rows[rows(planes + b, sub), :]
            weight = weight_lanes[s, here, :1]
            gap = jnp.zeros((sub, lanes), f32)
            for q in range(books):
                hit = positions == target_lanes[s, here, q : q + 1]
                teacher_logp = (scaled[q, here, :] - teacher_side[:, q : q + 1]).astype(bf16).astype(f32)
                mentor = jnp.exp(teacher_logp)
                u = logits[q, here, :]
                warmed = u / sharpness_divisor - student_side[:, pitch + q : pitch + q + 1]
                untempered = u - student_side[:, q : q + 1]
                value = jnp.sum(mentor * (teacher_logp - warmed), axis=1, keepdims=True)
                gap = jnp.where(lane == 2 * pitch + q, value, gap)
                slope = weight * (
                    blend_ratio * sharpness_divisor * (jnp.exp(warmed) - mentor)
                    + (1.0 - blend_ratio) * (jnp.exp(untempered) - jnp.where(hit, 1.0, 0.0))
                )
                slopes_all[
                    s, rows(me * planes + b, sub), q * columns : (q + 1) * columns
                ] = slope.astype(bf16)
            gaps[b, rows(s, sub), :] = gap

        over(planes, slope_rows)
        for index, shift in enumerate(faces + cores):
            slope_copy(s, me, index, peer(shift)).start()

    def relay_slopes(s):
        for n, shift in enumerate(faces):
            source = place_of(peer(shift, -1))
            slope_copy(s, source, 0, (role, dp)).wait_recv()
            for m, turn in enumerate(cores):
                index = len(faces) + len(cores) + n * len(cores) + m
                slope_copy(s, source, index, peer(turn)).start()

    def add_gradient(s):
        for n in range(1, places):
            feature_copy(s, n, True).wait_recv()
            if shifts[n][2]:
                slope_copy(s, place_of(peer(shifts[n], -1)), 0, (role, dp)).wait_recv()

        def book(q):
            out[q] = out[q] + lax.dot_general(
                features_all[s],
                slopes_all[s, :, rows(q, columns)],
                (((0,), (0,)), ((), ())),
                preferred_element_type=f32,
            )

        over(books, book)

    barrier = pltpu.get_barrier_semaphore()

    def greet(step, carry):
        other = lax.rem(plane + step, planes)
        pl.semaphore_signal(barrier, inc=1, device_id=(role, dp, other), device_id_type=MESH)
        return carry

    lax.fori_loop(1, planes, greet, 0)
    for shift in shifts[1:]:
        r, d = peer(shift)
        pl.semaphore_signal(barrier, inc=1, device_id=(r, d, plane), device_id_type=MESH)
    pl.semaphore_wait(barrier, planes - 1 + places - 1)

    def send_packed(step, carry):
        packed_copy(step, False).start()
        return carry

    lax.fori_loop(1, planes, send_packed, 0)
    for s in range(min(2, rounds)):
        for kind in range(2):
            send_own(kind, s)
    for kind in range(2):
        over(rounds, lambda s: own_local(kind, s).start())
    for kind in range(2):
        over(books, lambda q: weight_copy(kind, q).start())

    packed[plane] = packed_in[...]

    def clear(q):
        out[q] = jnp.zeros(out.shape[1:], f32)

    over(books, clear)

    def packed_arrive(step, carry):
        packed_copy(step, True).wait_recv()
        return carry

    lax.fori_loop(1, planes, packed_arrive, 0)
    length = packed.shape[2]
    picks = (
        lax.broadcasted_iota(jnp.int32, (half, length), 1)
        == lax.broadcasted_iota(jnp.int32, (half, length), 0) + role * half
    )

    def unpack(b):
        block = packed[b].astype(f32)

        def column(k):
            return jnp.sum(jnp.where(picks, block[k : k + 1, :], 0.0), axis=1, keepdims=True)

        lane = lane_of(half)
        ids = jnp.zeros((half, lanes), jnp.int32)
        for q in range(books):
            ids = jnp.where(lane == q, column(q).astype(jnp.int32) - plane * columns, ids)
        document = column(books)

        def count(p, total):
            same = document == packed[p].astype(f32)[books : books + 1, :]
            return total + jnp.sum(jnp.where(same, 1.0, 0.0), axis=1, keepdims=True)

        size = lax.fori_loop(0, planes, count, jnp.zeros((half, 1), f32))
        weight = jnp.broadcast_to((planes * length) / ((2 * planes) * size), (half, lanes))
        for s in range(rounds):
            target_lanes[s, rows(b, sub), :] = ids[s * sub : (s + 1) * sub]
            weight_lanes[s, rows(b, sub), :] = weight[s * sub : (s + 1) * sub]

    over(planes, unpack)

    forward(0)

    def iteration(s):
        @pl.when(s + 1 < rounds)
        def _():
            forward(s + 1)

        @pl.when(jnp.logical_and(s >= 1, s <= rounds))
        def _():
            compute_slopes(s - 1)

        @pl.when(s < rounds)
        def _():
            compute_logits(s)

        @pl.when(s >= 2)
        def _():
            add_gradient(s - 2)

        @pl.when(jnp.logical_and(s >= 1, s <= rounds))
        def _():
            relay_slopes(s - 1)

        @pl.when(s == rounds)
        def _():
            def send_gaps(step, carry):
                gap_copy(step, False).start()
                return carry

            lax.fori_loop(1, planes, send_gaps, 0)

    over(rounds + 2, iteration)

    def add_gap(step, total):
        gap_copy(step, True).wait_recv()
        return total + gaps_in[lax.rem(plane + planes - step, planes)]

    gap_total = lax.fori_loop(1, planes, add_gap, gaps[plane])
    student_terms = (
        blend_ratio * sharpness_divisor * sharpness_divisor * gap_total + (1.0 - blend_ratio) * own_terms[1]
    )
    teacher_terms = own_terms[0]
    mine = jnp.where(role == 0, teacher_terms, student_terms)
    swap[...] = jnp.where(role == 0, student_terms, teacher_terms)
    exchange = remote(swap, terms_out.at[role], swap_sem.at[0], swap_sem.at[1], (1 - role, dp, plane))
    exchange.start()
    terms_out[role] = mine
    exchange.wait_send()
    remote(swap, terms_out.at[1 - role], swap_sem.at[0], swap_sem.at[1], (1 - role, dp, plane)).wait_recv()

    def drain_line(step, carry):
        packed_copy(step, False).wait_send()
        gap_copy(step, False).wait_send()
        over(rounds, lambda s: stats_copy(s, step, False).wait_send())
        return carry

    lax.fori_loop(1, planes, drain_line, 0)

    def drain_round(s):
        for n in range(1, places):
            feature_copy(s, n, False).wait_send()
        for index in range(len(faces) + len(cores) + len(faces) * len(cores)):
            slope_copy(s, me, index, (role, dp)).wait_send()

        def drain_block(b):
            for kind in range(2):

                @pl.when(jnp.logical_and(b <= plane, plane < planes - 1))
                def _():
                    z_copy(kind, s, b, True, False).wait_send()

                @pl.when(jnp.logical_and(b >= plane, plane > 0))
                def _():
                    z_copy(kind, s, b, False, False).wait_send()

        over(planes, drain_block)

    over(rounds, drain_round)


def on_device(
    teacher_states,
    student_states,
    teacher_gain,
    student_gain,
    mentor_output_weights,
    student_heads,
    segments,
    targets,
):
    books, teacher_width, columns = mentor_output_weights.shape
    student_width = student_heads.shape[1]
    roles, dps, planes = (lax.axis_size(name) for name in ("role", "dp", "ctx"))
    inner = 2 if dps % 2 == 0 else 1
    places = roles * dps
    rows_here = teacher_states.shape[1]
    half = rows_here // roles
    rounds = half // sub
    group = planes * sub
    share = student_width // places
    sizes = (roles, dps, planes, inner, books, columns, share, half)

    packed = jnp.concatenate([targets[0].T, segments], axis=0)
    packed = jnp.pad(packed, ((0, pitch - books - 1), (0, 0)))

    vmem = pl.BlockSpec(memory_space=pltpu.VMEM)
    hbm = pl.BlockSpec(memory_space=pltpu.HBM)
    dma = pltpu.SemaphoreType.DMA
    shares, terms = pl.pallas_call(
        functools.partial(kernel, sizes),
        out_shape=(
            jax.ShapeDtypeStruct((books, share, columns), f32),
            jax.ShapeDtypeStruct((roles, half, lanes), f32),
        ),
        in_specs=[hbm, hbm, vmem, vmem, hbm, hbm, vmem],
        out_specs=(vmem, vmem),
        scratch_shapes=[
            pltpu.VMEM((rounds, planes, sub, teacher_width), bf16),
            pltpu.VMEM((rounds, planes, sub, student_width), bf16),
            pltpu.VMEM(mentor_output_weights.shape, bf16),
            pltpu.VMEM(student_heads.shape, bf16),
            pltpu.VMEM((group, teacher_width), bf16),
            pltpu.VMEM((group, student_width), bf16),
            pltpu.VMEM((rounds, places, group, share), bf16),
            pltpu.VMEM((rounds, places * group, share), bf16),
            pltpu.VMEM((rounds, places * group, books * columns), bf16),
            pltpu.VMEM((books, group, columns), f32),
            pltpu.VMEM((books, group, columns), f32),
            pltpu.VMEM((planes, pitch, rows_here), jnp.int32),
            pltpu.VMEM((rounds, group, lanes), jnp.int32),
            pltpu.VMEM((rounds, group, lanes), f32),
            pltpu.VMEM((2 * group, lanes), f32),
            pltpu.VMEM((rounds, planes, 4 * pitch, 2 * group), f32),
            pltpu.VMEM((2 * group, lanes), f32),
            pltpu.VMEM((planes, half, lanes), f32),
            pltpu.VMEM((planes, half, lanes), f32),
            pltpu.VMEM((2, half, lanes), f32),
            pltpu.VMEM((half, lanes), f32),
            dma((2, 2, rounds, planes)),
            dma((2, rounds, planes)),
            dma((2, rounds)),
            dma((2, books)),
            dma((planes,)),
            dma((planes,)),
            dma((rounds, planes)),
            dma((rounds, planes)),
            dma((rounds, places)),
            dma((rounds, places)),
            dma((rounds, places)),
            dma((rounds, places)),
            dma((planes,)),
            dma((planes,)),
            dma((2,)),
        ],
        compiler_params=pltpu.CompilerParams(
            collective_id=0, has_side_effects=True, vmem_limit_bytes=67_043_328
        ),
        name="distill",
    )(
        teacher_states[0],
        student_states[0],
        teacher_gain[None],
        student_gain[None],
        mentor_output_weights,
        student_heads,
        packed,
    )
    frame_terms = terms[:, :, 2 * pitch : 2 * pitch + books]
    return shares, frame_terms.reshape(1, 1, rows_here, books)


def solution(mesh):
    return jax.shard_map(
        on_device,
        mesh=mesh,
        in_specs=(
            P("dp", "ctx", None),
            P("dp", "ctx", None),
            P(),
            P(),
            P(None, None, "ctx"),
            P(None, None, "ctx"),
            P("dp", "ctx"),
            P("dp", "ctx", None),
        ),
        out_specs=(P(None, ("role", "dp"), "ctx"), P("role", "dp", "ctx", None)),
        check_vma=False,
    )
```

profile of v0, /device:TPU:0, one launch (start us, length us, event | category | flops | bytes accessed | tf_op | source)
XLA Modules:
  0.0 147.1 jit_solution(6557092282546691210)
XLA Ops:
  0.6 0.7 pad_add_fusion
  1.3 0.6 pad.4.packed_in
  1.9 1.3 broadcast_in_dim.7.student_gain
  3.3 138.0 %distill.1 = (f32[4,448,512]{2,1,0:T(8,128)}, f32[2,64,128]{2,1,0:T(8,128)}) custom-call(bf16[128,5120]{1,0:T(8,128)(2,1)} %bitcast.7, bf16[128,3584]{1,0:T(8,128)(2,1)} %bitcast.8, f32[1,5120]{1,0:T(1,128)} %bitcast.10, f32[1,3584]{1,0:T(1,128)} %broadcast_in_dim.7.student_gain, bf16[4,5120,512]{2,1,0:T(8,128)(2,1)} %teacher_weights_in.1, ...), custom_call_target="tpu_custom_call" | custom-call | tf_op jit(solution)/shard_map/distill/pallas_call | solution.py:572
  141.2 0.9 slice.3
  142.2 0.7 copy.10
  142.8 4.2 %copy.12 = f32[4,448,512]{2,1,0:T(8,128)} copy(f32[4,448,512]{2,1,0:T(8,128)} %get-tuple-element.10) | data formatting | bytes 7340032
where the time goes:
time: 147 us
  Pallas kernels  138 us (94%)
  local copies, waits for them, and re-layouts  7.74 us (5%)
    pallas_call x1, Pallas kernels, on_device(): pl.pallas_call(functools.partial(kernel, sizes), out_shape=(jax.ShapeDtyp...  138 us
    unnamed x2, local copies, waits for them, and re-layouts  4.91 us

commit v1 on v0

--- a/solution.py
+++ b/solution.py
@@ -21,15 +21,15 @@
 
 
 def normalize_rows(source, gain, target, width):
-    step = 512 if width % 512 == 0 else 128
-    total = jnp.zeros((sub, step), f32)
-    for start in range(0, width, step):
-        x = source[:, start : start + step].astype(f32)
-        total = total + x * x
+    parts = [jnp.zeros((sub, lanes), f32) for _ in range(4)]
+    for k in range(width // lanes):
+        x = source[:, k * lanes : (k + 1) * lanes].astype(f32)
+        parts[k % 4] = parts[k % 4] + x * x
+    total = (parts[0] + parts[1]) + (parts[2] + parts[3])
     factor = lax.rsqrt(jnp.sum(total, axis=1, keepdims=True) / width + epsilon)
-    for start in range(0, width, step):
-        x = source[:, start : start + step].astype(f32)
-        target[:, start : start + step] = (x * factor * gain[:, start : start + step]).astype(bf16)
+    for k in range(width // lanes):
+        x = source[:, k * lanes : (k + 1) * lanes].astype(f32)
+        target[:, k * lanes : (k + 1) * lanes] = (x * factor * gain[k : k + 1, :]).astype(bf16)
 
 
 def kernel(
@@ -40,7 +40,8 @@
     student_gain,
     teacher_weights_in,
     student_weights_in,
-    packed_in,
+    targets_in,
+    segments_in,
     out,
     terms_out,
     teacher_raw,
@@ -54,7 +55,8 @@
     slopes_all,
     scaled,
     logits,
-    packed,
+    targets_all,
+    segments_all,
     target_lanes,
     weight_lanes,
     stat_rows,
@@ -64,6 +66,7 @@
     gaps_in,
     own_terms,
     swap,
+    both_terms,
     z_send,
     z_recv,
     z_local,
@@ -115,52 +118,69 @@
             src_ref=src, dst_ref=dst, send_sem=send, recv_sem=recv, device_id=device, device_id_type=MESH
         )
 
-    def z_copy(kind, s, b, up, own):
+    first, last = plane == 0, plane == planes - 1
+    skips = planes > 2
+
+    def z_copy(kind, s, b, up, own, distance=1):
         src = inputs[kind].at[rows(role * rounds + s, sub)] if own else raws[kind].at[s, b]
-        target = plane + 1 if up else plane - 1
+        target = plane + distance if up else plane - distance
+        slot = int(up) if distance == 1 else 1 - int(up)
         return remote(
-            src, raws[kind].at[s, b], z_send.at[int(up), kind, s, b], z_recv.at[kind, s, b], (role, dp, target)
+            src, raws[kind].at[s, b], z_send.at[slot, kind, s, b], z_recv.at[kind, s, b], (role, dp, target)
         )
 
+    def passes(b, up):
+        ahead = b < plane if up else b > plane
+        inside = plane < planes - 1 if up else plane > 0
+        edge = 0 if up else planes - 1
+        direct = jnp.logical_and(b == edge, plane == (1 if up else planes - 2))
+        relayed = jnp.logical_and(ahead, jnp.logical_not(direct)) if skips else ahead
+        return jnp.logical_and(inside, relayed)
+
     def send_own(kind, s):
-        @pl.when(plane < planes - 1)
+        @pl.when(jnp.logical_not(last))
         def _():
             z_copy(kind, s, plane, True, True).start()
 
-        @pl.when(plane > 0)
+        @pl.when(jnp.logical_not(first))
         def _():
             z_copy(kind, s, plane, False, True).start()
+
+        if skips:
+
+            @pl.when(first)
+            def _():
+                z_copy(kind, s, plane, True, True, 2).start()
+
+            @pl.when(last)
+            def _():
+                z_copy(kind, s, plane, False, True, 2).start()
 
     def z_arrive(kind, s, b):
         z_copy(kind, s, b, True, False).wait_recv()
 
-    def pass_on(kind, s, hop):
-        @pl.when(jnp.logical_and(middle, plane - hop >= 0))
-        def _():
-            b = plane - hop
-            z_arrive(kind, s, b)
-            z_copy(kind, s, b, True, False).start()
-
-        @pl.when(jnp.logical_and(middle, plane + hop <= planes - 1))
-        def _():
-            b = plane + hop
-            z_arrive(kind, s, b)
-            z_copy(kind, s, b, False, False).start()
+    def pass_on(kind, s, b, up):
+        z_arrive(kind, s, b)
+
+        @pl.when(passes(b, up))
+        def _():
+            z_copy(kind, s, b, up, False).start()
 
     def forward(s):
         for kind in range(2):
-            pass_on(kind, s, 1)
-
-            @pl.when(s + 2 < rounds)
-            def _():
-                send_own(kind, s + 2)
 
             def hops(h, carry):
-                pass_on(kind, s, h)
+                @pl.when(plane - h >= 0)
+                def _():
+                    pass_on(kind, s, plane - h, True)
+
+                @pl.when(plane + h <= planes - 1)
+                def _():
+                    pass_on(kind, s, plane + h, False)
+
                 return carry
 
-            if planes > 2:
-                lax.fori_loop(2, planes, hops, 0)
+            lax.fori_loop(1, planes, hops, 0)
 
     def own_local(kind, s):
         return pltpu.make_async_copy(
@@ -171,16 +191,13 @@
         src, dst = ((teacher_weights_in, teacher_weights), (student_weights_in, student_weights))[kind]
         return pltpu.make_async_copy(src.at[q], dst.at[q], weights_sem.at[kind, q])
 
-    def packed_copy(step, arriving):
+    labels = ((targets_in, targets_all), (segments_in, segments_all))
+
+    def label_copy(n, step, arriving):
         other = lax.rem(plane + (planes - step if arriving else step), planes)
         slot = other if arriving else plane
-        return remote(
-            packed.at[slot] if arriving else packed_in,
-            packed.at[slot],
-            packed_send.at[step],
-            packed_recv.at[slot],
-            (role, dp, other),
-        )
+        source, there = labels[n]
+        return remote(source, there.at[slot], packed_send.at[n, step], packed_recv.at[n, slot], (role, dp, other))
 
     def stats_copy(s, step, arriving):
         other = lax.rem(plane + (planes - step if arriving else step), planes)
@@ -208,12 +225,30 @@
             (where[0], where[1], plane),
         )
 
-    def slope_copy(s, source, index, where):
-        part = slopes_all.at[s, rows(source, group)]
-        return remote(part, part, slope_send.at[s, index], slope_recv.at[s, source], (where[0], where[1], plane))
-
-    faces = [(dr, do, 0) for dr, do in itertools.product(range(roles), range(outer)) if dr or do]
-    cores = [(0, 0, di) for di in range(1, inner)]
+    part_rows = group // 2
+
+    def slope_copy(s, source, part, index, where):
+        piece = slopes_all.at[s, rows(source * 2 + part, part_rows)]
+        return remote(
+            piece, piece, slope_send.at[s, index], slope_recv.at[s, source, part], (where[0], where[1], plane)
+        )
+
+    turns = [(0, 0, di) for di in range(1, inner)]
+    across = [(dr, 0, 0) for dr in range(1, roles)]
+    along = [(0, do, 0) for do in range(1, outer)]
+    corners = [(dr, do, 0) for dr in range(1, roles) for do in range(1, outer)]
+    own_sends = (
+        [(t, 0) for t in across]
+        + [(t, 1) for t in along]
+        + [(t, 1) for t in across]
+        + [(t, 0) for t in along]
+        + [(t, h) for h in range(2) for t in turns]
+    )
+    slope_sends = (
+        len(own_sends)
+        + 2 * len(corners)
+        + 2 * (len(across) + len(along) + len(corners)) * len(turns)
+    )
 
     def over(count, body):
         def step(i, carry):
@@ -366,22 +401,40 @@
             gaps[b, rows(s, sub), :] = gap
 
         over(planes, slope_rows)
-        for index, shift in enumerate(faces + cores):
-            slope_copy(s, me, index, peer(shift)).start()
+        for index, (turn, part) in enumerate(own_sends):
+            slope_copy(s, me, part, index, peer(turn)).start()
 
     def relay_slopes(s):
-        for n, shift in enumerate(faces):
-            source = place_of(peer(shift, -1))
-            slope_copy(s, source, 0, (role, dp)).wait_recv()
-            for m, turn in enumerate(cores):
-                index = len(faces) + len(cores) + n * len(cores) + m
-                slope_copy(s, source, index, peer(turn)).start()
+        index = len(own_sends)
+        for lead in range(2):
+            for turn in across + along:
+                part = lead if turn in across else 1 - lead
+                source = place_of(peer(turn, -1))
+                slope_copy(s, source, part, 0, (role, dp)).wait_recv()
+                if lead == 0:
+                    for onward in along if turn in across else across:
+                        slope_copy(s, source, part, index, peer(onward)).start()
+                        index += 1
+                for flip in turns:
+                    slope_copy(s, source, part, index, peer(flip)).start()
+                    index += 1
+
+    def share_corners(s):
+        index = slope_sends - 2 * len(corners) * len(turns)
+        for turn in corners:
+            source = place_of(peer(turn, -1))
+            for part in range(2):
+                slope_copy(s, source, part, 0, (role, dp)).wait_recv()
+                for flip in turns:
+                    slope_copy(s, source, part, index, peer(flip)).start()
+                    index += 1
 
     def add_gradient(s):
         for n in range(1, places):
             feature_copy(s, n, True).wait_recv()
             if shifts[n][2]:
-                slope_copy(s, place_of(peer(shifts[n], -1)), 0, (role, dp)).wait_recv()
+                for part in range(2):
+                    slope_copy(s, place_of(peer(shifts[n], -1)), part, 0, (role, dp)).wait_recv()
 
         def book(q):
             out[q] = out[q] + lax.dot_general(
@@ -406,11 +459,12 @@
         pl.semaphore_signal(barrier, inc=1, device_id=(r, d, plane), device_id_type=MESH)
     pl.semaphore_wait(barrier, planes - 1 + places - 1)
 
-    def send_packed(step, carry):
-        packed_copy(step, False).start()
+    def send_labels(step, carry):
+        for n in range(2):
+            label_copy(n, step, False).start()
         return carry
 
-    lax.fori_loop(1, planes, send_packed, 0)
+    lax.fori_loop(1, planes, send_labels, 0)
     for s in range(min(2, rounds)):
         for kind in range(2):
             send_own(kind, s)
@@ -419,38 +473,40 @@
     for kind in range(2):
         over(books, lambda q: weight_copy(kind, q).start())
 
-    packed[plane] = packed_in[...]
+    targets_all[plane] = targets_in[...]
+    segments_all[plane] = segments_in[...]
 
     def clear(q):
         out[q] = jnp.zeros(out.shape[1:], f32)
 
     over(books, clear)
 
-    def packed_arrive(step, carry):
-        packed_copy(step, True).wait_recv()
+    def labels_arrive(step, carry):
+        for n in range(2):
+            label_copy(n, step, True).wait_recv()
         return carry
 
-    lax.fori_loop(1, planes, packed_arrive, 0)
-    length = packed.shape[2]
+    lax.fori_loop(1, planes, labels_arrive, 0)
+    length = segments_all.shape[2]
     picks = (
         lax.broadcasted_iota(jnp.int32, (half, length), 1)
         == lax.broadcasted_iota(jnp.int32, (half, length), 0) + role * half
     )
 
     def unpack(b):
-        block = packed[b].astype(f32)
-
-        def column(k):
-            return jnp.sum(jnp.where(picks, block[k : k + 1, :], 0.0), axis=1, keepdims=True)
+        block = targets_all[b].astype(f32)
+
+        def column(line):
+            return jnp.sum(jnp.where(picks, line, 0.0), axis=1, keepdims=True)
 
         lane = lane_of(half)
         ids = jnp.zeros((half, lanes), jnp.int32)
         for q in range(books):
-            ids = jnp.where(lane == q, column(q).astype(jnp.int32) - plane * columns, ids)
-        document = column(books)
+            ids = jnp.where(lane == q, column(block[q : q + 1, :]).astype(jnp.int32) - plane * columns, ids)
+        document = column(segments_all[b].astype(f32))
 
         def count(p, total):
-            same = document == packed[p].astype(f32)[books : books + 1, :]
+            same = document == segments_all[p].astype(f32)
             return total + jnp.sum(jnp.where(same, 1.0, 0.0), axis=1, keepdims=True)
 
         size = lax.fori_loop(0, planes, count, jnp.zeros((half, 1), f32))
@@ -461,28 +517,41 @@
 
     over(planes, unpack)
 
-    forward(0)
+    def owns(s):
+        for kind in range(2):
+            send_own(kind, s)
+
+    def between(low, s, high, also=True):
+        return jnp.logical_and(jnp.logical_and(s >= low, s < high), also)
 
     def iteration(s):
-        @pl.when(s + 1 < rounds)
-        def _():
-            forward(s + 1)
-
-        @pl.when(jnp.logical_and(s >= 1, s <= rounds))
+        @pl.when(between(0, s, rounds, middle))
+        def _():
+            forward(s)
+
+        @pl.when(between(1, s, rounds - 1, middle))
+        def _():
+            owns(s + 1)
+
+        @pl.when(between(1, s, rounds + 1))
         def _():
             compute_slopes(s - 1)
 
-        @pl.when(s < rounds)
+        @pl.when(between(0, s, rounds))
         def _():
             compute_logits(s)
 
-        @pl.when(s >= 2)
-        def _():
-            add_gradient(s - 2)
-
-        @pl.when(jnp.logical_and(s >= 1, s <= rounds))
-        def _():
-            relay_slopes(s - 1)
+        @pl.when(between(0, s, rounds - 2, jnp.logical_not(middle)))
+        def _():
+            owns(s + 2)
+
+        @pl.when(between(2, s, rounds + 2))
+        def _():
+            share_corners(s - 2)
+
+        @pl.when(between(3, s, rounds + 3))
+        def _():
+            add_gradient(s - 3)
 
         @pl.when(s == rounds)
         def _():
@@ -492,7 +561,11 @@
 
             lax.fori_loop(1, planes, send_gaps, 0)
 
-    over(rounds + 2, iteration)
+        @pl.when(between(1, s, rounds + 1))
+        def _():
+            relay_slopes(s - 1)
+
+    over(rounds + 3, iteration)
 
     def add_gap(step, total):
         gap_copy(step, True).wait_recv()
@@ -505,14 +578,15 @@
     teacher_terms = own_terms[0]
     mine = jnp.where(role == 0, teacher_terms, student_terms)
     swap[...] = jnp.where(role == 0, student_terms, teacher_terms)
-    exchange = remote(swap, terms_out.at[role], swap_sem.at[0], swap_sem.at[1], (1 - role, dp, plane))
+    exchange = remote(swap, both_terms.at[rows(role, half)], swap_sem.at[0], swap_sem.at[1], (1 - role, dp, plane))
     exchange.start()
-    terms_out[role] = mine
-    exchange.wait_send()
-    remote(swap, terms_out.at[1 - role], swap_sem.at[0], swap_sem.at[1], (1 - role, dp, plane)).wait_recv()
+    both_terms[rows(role, half), :] = mine
+    exchange.wait()
+    terms_out[...] = jnp.transpose(both_terms[...])[2 * pitch : 2 * pitch + books]
 
     def drain_line(step, carry):
-        packed_copy(step, False).wait_send()
+        for n in range(2):
+            label_copy(n, step, False).wait_send()
         gap_copy(step, False).wait_send()
         over(rounds, lambda s: stats_copy(s, step, False).wait_send())
         return carry
@@ -522,17 +596,21 @@
     def drain_round(s):
         for n in range(1, places):
             feature_copy(s, n, False).wait_send()
-        for index in range(len(faces) + len(cores) + len(faces) * len(cores)):
-            slope_copy(s, me, index, (role, dp)).wait_send()
+        for index in range(slope_sends):
+            slope_copy(s, me, 0, index, (role, dp)).wait_send()
 
         def drain_block(b):
             for kind in range(2):
 
-                @pl.when(jnp.logical_and(b <= plane, plane < planes - 1))
+                own = b == plane
+                up = jnp.logical_or(passes(b, True), own if skips else jnp.logical_and(own, jnp.logical_not(last)))
+                down = jnp.logical_or(passes(b, False), own if skips else jnp.logical_and(own, jnp.logical_not(first)))
+
+                @pl.when(up)
                 def _():
                     z_copy(kind, s, b, True, False).wait_send()
 
-                @pl.when(jnp.logical_and(b >= plane, plane > 0))
+                @pl.when(down)
                 def _():
                     z_copy(kind, s, b, False, False).wait_send()
 
@@ -563,9 +641,6 @@
     share = student_width // places
     sizes = (roles, dps, planes, inner, books, columns, share, half)
 
-    packed = jnp.concatenate([targets[0].T, segments], axis=0)
-    packed = jnp.pad(packed, ((0, pitch - books - 1), (0, 0)))
-
     vmem = pl.BlockSpec(memory_space=pltpu.VMEM)
     hbm = pl.BlockSpec(memory_space=pltpu.HBM)
     dma = pltpu.SemaphoreType.DMA
@@ -573,9 +648,9 @@
         functools.partial(kernel, sizes),
         out_shape=(
             jax.ShapeDtypeStruct((books, share, columns), f32),
-            jax.ShapeDtypeStruct((roles, half, lanes), f32),
+            jax.ShapeDtypeStruct((books, rows_here), f32),
         ),
-        in_specs=[hbm, hbm, vmem, vmem, hbm, hbm, vmem],
+        in_specs=[hbm, hbm, vmem, vmem, hbm, hbm, vmem, vmem],
         out_specs=(vmem, vmem),
         scratch_shapes=[
             pltpu.VMEM((rounds, planes, sub, teacher_width), bf16),
@@ -589,7 +664,8 @@
             pltpu.VMEM((rounds, places * group, books * columns), bf16),
             pltpu.VMEM((books, group, columns), f32),
             pltpu.VMEM((books, group, columns), f32),
-            pltpu.VMEM((planes, pitch, rows_here), jnp.int32),
+            pltpu.VMEM((planes, books, rows_here), jnp.int32),
+            pltpu.VMEM((planes, 1, rows_here), jnp.int32),
             pltpu.VMEM((rounds, group, lanes), jnp.int32),
             pltpu.VMEM((rounds, group, lanes), f32),
             pltpu.VMEM((2 * group, lanes), f32),
@@ -599,18 +675,19 @@
             pltpu.VMEM((planes, half, lanes), f32),
             pltpu.VMEM((2, half, lanes), f32),
             pltpu.VMEM((half, lanes), f32),
+            pltpu.VMEM((rows_here, lanes), f32),
             dma((2, 2, rounds, planes)),
             dma((2, rounds, planes)),
             dma((2, rounds)),
             dma((2, books)),
-            dma((planes,)),
-            dma((planes,)),
+            dma((2, planes)),
+            dma((2, planes)),
             dma((rounds, planes)),
             dma((rounds, planes)),
             dma((rounds, places)),
             dma((rounds, places)),
-            dma((rounds, places)),
-            dma((rounds, places)),
+            dma((rounds, 4 * places)),
+            dma((rounds, places, 2)),
             dma((planes,)),
             dma((planes,)),
             dma((2,)),
@@ -622,14 +699,14 @@
     )(
         teacher_states[0],
         student_states[0],
-        teacher_gain[None],
-        student_gain[None],
+        teacher_gain.reshape(-1, lanes),
+        student_gain.reshape(-1, lanes),
         mentor_output_weights,
         student_heads,
-        packed,
+        targets[0].T,
+        segments,
     )
-    frame_terms = terms[:, :, 2 * pitch : 2 * pitch + books]
-    return shares, frame_terms.reshape(1, 1, rows_here, books)
+    return shares, terms.T.reshape(1, 1, rows_here, books)
 
 
 def solution(mesh):

time: 147 us -> 124 us (0.84)
  Pallas kernels: 138 us -> 118 us
  local copies, waits for them, and re-layouts: 7.74 us -> 4.83 us
    pallas_call x1, Pallas kernels: 138 us -> 118 us  [on_device(): pl.pallas_call(functools.partial(kernel, sizes), out_shape=(jax.ShapeDtyp...]
    unnamed x2 -> x4, local copies, waits for them, and re-layouts: 4.91 us -> 4.83 us
where the time goes in v1:
time: 124 us
  Pallas kernels  118 us (95%)
  local copies, waits for them, and re-layouts  4.83 us (4%)
    pallas_call x1, Pallas kernels, on_device(): pl.pallas_call(functools.partial(kernel, sizes), out_shape=(jax.ShapeDtyp...  118 us
    unnamed x4, local copies, waits for them, and re-layouts  4.83 us

profile of v1, /device:TPU:0, one launch (start us, length us, event | category | flops | bytes accessed | tf_op | source)
XLA Modules:
  0.0 123.8 jit_solution(14263629357174784026)
XLA Ops:
  0.6 118.3 %distill.1 = (f32[4,448,512]{2,1,0:T(8,128)}, f32[4,128]{1,0:T(4,128)}) custom-call(bf16[128,5120]{1,0:T(8,128)(2,1)} %bitcast.10, bf16[128,3584]{1,0:T(8,128)(2,1)} %bitcast.11, f32[40,128]{1,0:T(8,128)} %bitcast.12, f32[28,128]{1,0:T(8,128)} %bitcast.13, bf16[4,5120,512]{2,1,0:T(8,128)(2,1)} %teacher_weights_in.1, ...), custom_call_target="tpu_custom_call" | custom-call | tf_op jit(solution)/shard_map/distill/pallas_call | solution.py:647
  118.9 0.0 copy-start
  118.9 4.2 %copy.12 = f32[4,448,512]{2,1,0:T(8,128)} copy(f32[4,448,512]{2,1,0:T(8,128)} %get-tuple-element.8) | data formatting | bytes 7340032
  123.2 0.0 copy-done
  123.2 0.6 copy.13
Async XLA Ops:
  118.9 4.3 %copy-start = (f32[4,128]{1,0:T(4,128)S(1)}, f32[4,128]{1,0:T(4,128)}, u32[]{:S(2)}) copy-start(f32[4,128]{1,0:T(4,128)} %get-tuple-element.5) | copy-start | bytes 6148

commit v2 on v1

--- a/solution.py
+++ b/solution.py
@@ -57,8 +57,7 @@
     logits,
     targets_all,
     segments_all,
-    target_lanes,
-    weight_lanes,
+    frame_lanes,
     stat_rows,
     stats,
     norm_rows,
@@ -67,6 +66,7 @@
     own_terms,
     swap,
     both_terms,
+    features_turned,
     z_send,
     z_recv,
     z_local,
@@ -166,21 +166,19 @@
         def _():
             z_copy(kind, s, b, up, False).start()
 
-    def forward(s):
-        for kind in range(2):
-
-            def hops(h, carry):
-                @pl.when(plane - h >= 0)
-                def _():
-                    pass_on(kind, s, plane - h, True)
-
-                @pl.when(plane + h <= planes - 1)
-                def _():
-                    pass_on(kind, s, plane + h, False)
-
-                return carry
-
-            lax.fori_loop(1, planes, hops, 0)
+    def forward(kind, s):
+        def hops(h, carry):
+            @pl.when(plane - h >= 0)
+            def _():
+                pass_on(kind, s, plane - h, True)
+
+            @pl.when(plane + h <= planes - 1)
+            def _():
+                pass_on(kind, s, plane + h, False)
+
+            return carry
+
+        lax.fori_loop(1, planes, hops, 0)
 
     def own_local(kind, s):
         return pltpu.make_async_copy(
@@ -284,9 +282,11 @@
 
     lane_of = lambda count: lax.broadcasted_iota(jnp.int32, (count, lanes), 1)
 
-    def compute_logits(s):
+    def teacher_logits(s):
         over(planes, lambda b: take(0, s, b))
         over(books, lambda q: project(0, s, q))
+
+    def student_logits(s):
         over(planes, lambda b: take(1, s, b))
 
         def cut(b):
@@ -294,12 +294,12 @@
                 slabs[s, p, rows(b, sub), :] = student_normed[rows(b, sub), p * share : (p + 1) * share]
 
         over(planes, cut)
+        for n in range(1, places):
+            feature_copy(s, n, False).start()
         features_all[s, rows(me, group), :] = slabs[s, me]
         over(books, lambda q: project(1, s, q))
-        for n in range(1, places):
-            feature_copy(s, n, False).start()
-
-        positions = lax.broadcasted_iota(jnp.int32, (sub, columns), 1)
+
+        positions = lax.broadcasted_iota(jnp.int32, (sub, columns), 1).astype(f32)
         lane = lane_of(sub)
 
         def totals(b):
@@ -307,7 +307,7 @@
             first = jnp.zeros((sub, lanes), f32)
             second = jnp.zeros((sub, lanes), f32)
             for q in range(books):
-                hit = positions == target_lanes[s, here, q : q + 1]
+                hit = positions == frame_lanes[s, here, q : q + 1]
 
                 def put(array, kind, value):
                     return jnp.where(lane == kind * pitch + q, value, array)
@@ -373,17 +373,17 @@
         own_terms[0, rows(s, sub), :] = norm_rows[rows(plane, sub), :]
         own_terms[1, rows(s, sub), :] = norm_rows[rows(planes + plane, sub), :]
 
-        positions = lax.broadcasted_iota(jnp.int32, (sub, columns), 1)
+        positions = lax.broadcasted_iota(jnp.int32, (sub, columns), 1).astype(f32)
         lane = lane_of(sub)
 
         def slope_rows(b):
             here = rows(b, sub)
             teacher_side = norm_rows[here, :]
             student_side = norm_rows[rows(planes + b, sub), :]
-            weight = weight_lanes[s, here, :1]
+            weight = frame_lanes[s, here, books : books + 1]
             gap = jnp.zeros((sub, lanes), f32)
             for q in range(books):
-                hit = positions == target_lanes[s, here, q : q + 1]
+                hit = positions == frame_lanes[s, here, q : q + 1]
                 teacher_logp = (scaled[q, here, :] - teacher_side[:, q : q + 1]).astype(bf16).astype(f32)
                 mentor = jnp.exp(teacher_logp)
                 u = logits[q, here, :]
@@ -436,12 +436,11 @@
                 for part in range(2):
                     slope_copy(s, place_of(peer(shifts[n], -1)), part, 0, (role, dp)).wait_recv()
 
+        features_turned[...] = jnp.transpose(features_all[s])
+
         def book(q):
-            out[q] = out[q] + lax.dot_general(
-                features_all[s],
-                slopes_all[s, :, rows(q, columns)],
-                (((0,), (0,)), ((), ())),
-                preferred_element_type=f32,
+            out[q] = out[q] + jnp.dot(
+                features_turned[...], slopes_all[s, :, rows(q, columns)], preferred_element_type=f32
             )
 
         over(books, book)
@@ -500,9 +499,10 @@
             return jnp.sum(jnp.where(picks, line, 0.0), axis=1, keepdims=True)
 
         lane = lane_of(half)
-        ids = jnp.zeros((half, lanes), jnp.int32)
+        facts = jnp.zeros((half, lanes), f32)
+        first_column = (plane * columns).astype(f32)
         for q in range(books):
-            ids = jnp.where(lane == q, column(block[q : q + 1, :]).astype(jnp.int32) - plane * columns, ids)
+            facts = jnp.where(lane == q, column(block[q : q + 1, :]) - first_column, facts)
         document = column(segments_all[b].astype(f32))
 
         def count(p, total):
@@ -510,10 +510,10 @@
             return total + jnp.sum(jnp.where(same, 1.0, 0.0), axis=1, keepdims=True)
 
         size = lax.fori_loop(0, planes, count, jnp.zeros((half, 1), f32))
-        weight = jnp.broadcast_to((planes * length) / ((2 * planes) * size), (half, lanes))
+        weight = (planes * length) / ((2 * planes) * size)
+        facts = jnp.where(lane == books, weight, facts)
         for s in range(rounds):
-            target_lanes[s, rows(b, sub), :] = ids[s * sub : (s + 1) * sub]
-            weight_lanes[s, rows(b, sub), :] = weight[s * sub : (s + 1) * sub]
+            frame_lanes[s, rows(b, sub), :] = facts[s * sub : (s + 1) * sub]
 
     over(planes, unpack)
 
@@ -524,34 +524,35 @@
     def between(low, s, high, also=True):
         return jnp.logical_and(jnp.logical_and(s >= low, s < high), also)
 
+    @pl.when(middle)
+    def _():
+        for kind in range(2):
+            forward(kind, 0)
+
     def iteration(s):
-        @pl.when(between(0, s, rounds, middle))
-        def _():
-            forward(s)
-
-        @pl.when(between(1, s, rounds - 1, middle))
-        def _():
-            owns(s + 1)
-
         @pl.when(between(1, s, rounds + 1))
         def _():
             compute_slopes(s - 1)
 
         @pl.when(between(0, s, rounds))
         def _():
-            compute_logits(s)
-
-        @pl.when(between(0, s, rounds - 2, jnp.logical_not(middle)))
+            teacher_logits(s)
+
+        @pl.when(between(0, s, rounds - 1, middle))
+        def _():
+            forward(0, s + 1)
+
+        @pl.when(between(0, s, rounds))
+        def _():
+            student_logits(s)
+
+        @pl.when(between(0, s, rounds - 1, middle))
+        def _():
+            forward(1, s + 1)
+
+        @pl.when(between(0, s, rounds - 2))
         def _():
             owns(s + 2)
-
-        @pl.when(between(2, s, rounds + 2))
-        def _():
-            share_corners(s - 2)
-
-        @pl.when(between(3, s, rounds + 3))
-        def _():
-            add_gradient(s - 3)
 
         @pl.when(s == rounds)
         def _():
@@ -560,6 +561,14 @@
                 return carry
 
             lax.fori_loop(1, planes, send_gaps, 0)
+
+        @pl.when(between(3, s, rounds + 3))
+        def _():
+            add_gradient(s - 3)
+
+        @pl.when(between(2, s, rounds + 2))
+        def _():
+            share_corners(s - 2)
 
         @pl.when(between(1, s, rounds + 1))
         def _():
@@ -647,7 +656,7 @@
     shares, terms = pl.pallas_call(
         functools.partial(kernel, sizes),
         out_shape=(
-            jax.ShapeDtypeStruct((books, share, columns), f32),
+            pltpu.VMEM((books, share, columns), f32),
             jax.ShapeDtypeStruct((books, rows_here), f32),
         ),
         in_specs=[hbm, hbm, vmem, vmem, hbm, hbm, vmem, vmem],
@@ -666,7 +675,6 @@
             pltpu.VMEM((books, group, columns), f32),
             pltpu.VMEM((planes, books, rows_here), jnp.int32),
             pltpu.VMEM((planes, 1, rows_here), jnp.int32),
-            pltpu.VMEM((rounds, group, lanes), jnp.int32),
             pltpu.VMEM((rounds, group, lanes), f32),
             pltpu.VMEM((2 * group, lanes), f32),
             pltpu.VMEM((rounds, planes, 4 * pitch, 2 * group), f32),
@@ -676,6 +684,7 @@
             pltpu.VMEM((2, half, lanes), f32),
             pltpu.VMEM((half, lanes), f32),
             pltpu.VMEM((rows_here, lanes), f32),
+            pltpu.VMEM((share, places * group), bf16),
             dma((2, 2, rounds, planes)),
             dma((2, rounds, planes)),
             dma((2, rounds)),
@@ -693,7 +702,7 @@
             dma((2,)),
         ],
         compiler_params=pltpu.CompilerParams(
-            collective_id=0, has_side_effects=True, vmem_limit_bytes=67_043_328
+            collective_id=0, has_side_effects=True, vmem_limit_bytes=67_043_328 - 4 * books * share * columns - (1 << 17)
         ),
         name="distill",
     )(

time: 124 us -> 117 us (0.944)
  Pallas kernels: 118 us -> 114 us
  local copies, waits for them, and re-layouts: 4.83 us -> 2.42 us
    pallas_call x1, Pallas kernels: 118 us -> 114 us  [on_device(): pl.pallas_call(functools.partial(kernel, sizes), out_shape=(pltpu.VMEM((b...]
    unnamed x4, local copies, waits for them, and re-layouts: 4.83 us -> 2.42 us
where the time goes in v2:
time: 117 us
  Pallas kernels  114 us (97%)
  local copies, waits for them, and re-layouts  2.42 us (2%)
    pallas_call x1, Pallas kernels, on_device(): pl.pallas_call(functools.partial(kernel, sizes), out_shape=(pltpu.VMEM((b...  114 us
    unnamed x4, local copies, waits for them, and re-layouts  2.42 us

profile of v2, /device:TPU:0, one launch (start us, length us, event | category | flops | bytes accessed | tf_op | source)
XLA Modules:
  0.0 116.7 jit_solution(15707284585870853306)
XLA Ops:
  0.6 113.6 %distill.1 = (f32[4,448,512]{2,1,0:T(8,128)S(1)}, f32[4,128]{1,0:T(4,128)}) custom-call(bf16[128,5120]{1,0:T(8,128)(2,1)} %bitcast.10, bf16[128,3584]{1,0:T(8,128)(2,1)} %bitcast.11, f32[40,128]{1,0:T(8,128)} %bitcast.12, f32[28,128]{1,0:T(8,128)} %bitcast.13, bf16[4,5120,512]{2,1,0:T(8,128)(2,1)} %teacher_weights_in.1, ...), custom_call_target="tpu_custom_call" | custom-call | tf_op jit(solution)/shard_map/distill/pallas_call | solution.py:656
  114.3 0.0 copy-start
  114.3 1.8 %copy.12 = f32[4,448,512]{2,1,0:T(8,128)} copy(f32[4,448,512]{2,1,0:T(8,128)S(1)} %get-tuple-element.6) | data formatting | bytes 7340032
  116.1 0.0 copy-done
  116.1 0.6 copy.13
Async XLA Ops:
  114.3 1.9 %copy-start = (f32[4,128]{1,0:T(4,128)S(1)}, f32[4,128]{1,0:T(4,128)}, u32[]{:S(2)}) copy-start(f32[4,128]{1,0:T(4,128)} %get-tuple-element.5) | copy-start | bytes 6148

commit v3 on v2

--- a/solution.py
+++ b/solution.py
@@ -57,7 +57,8 @@
     logits,
     targets_all,
     segments_all,
-    frame_lanes,
+    target_lanes,
+    weight_lanes,
     stat_rows,
     stats,
     norm_rows,
@@ -66,7 +67,6 @@
     own_terms,
     swap,
     both_terms,
-    features_turned,
     z_send,
     z_recv,
     z_local,
@@ -299,7 +299,7 @@
         features_all[s, rows(me, group), :] = slabs[s, me]
         over(books, lambda q: project(1, s, q))
 
-        positions = lax.broadcasted_iota(jnp.int32, (sub, columns), 1).astype(f32)
+        positions = lax.broadcasted_iota(jnp.int32, (sub, columns), 1)
         lane = lane_of(sub)
 
         def totals(b):
@@ -307,7 +307,7 @@
             first = jnp.zeros((sub, lanes), f32)
             second = jnp.zeros((sub, lanes), f32)
             for q in range(books):
-                hit = positions == frame_lanes[s, here, q : q + 1]
+                hit = positions == target_lanes[s, here, q : q + 1]
 
                 def put(array, kind, value):
                     return jnp.where(lane == kind * pitch + q, value, array)
@@ -373,17 +373,17 @@
         own_terms[0, rows(s, sub), :] = norm_rows[rows(plane, sub), :]
         own_terms[1, rows(s, sub), :] = norm_rows[rows(planes + plane, sub), :]
 
-        positions = lax.broadcasted_iota(jnp.int32, (sub, columns), 1).astype(f32)
+        positions = lax.broadcasted_iota(jnp.int32, (sub, columns), 1)
         lane = lane_of(sub)
 
         def slope_rows(b):
             here = rows(b, sub)
             teacher_side = norm_rows[here, :]
             student_side = norm_rows[rows(planes + b, sub), :]
-            weight = frame_lanes[s, here, books : books + 1]
+            weight = weight_lanes[s, here, :1]
             gap = jnp.zeros((sub, lanes), f32)
             for q in range(books):
-                hit = positions == frame_lanes[s, here, q : q + 1]
+                hit = positions == target_lanes[s, here, q : q + 1]
                 teacher_logp = (scaled[q, here, :] - teacher_side[:, q : q + 1]).astype(bf16).astype(f32)
                 mentor = jnp.exp(teacher_logp)
                 u = logits[q, here, :]
@@ -436,11 +436,12 @@
                 for part in range(2):
                     slope_copy(s, place_of(peer(shifts[n], -1)), part, 0, (role, dp)).wait_recv()
 
-        features_turned[...] = jnp.transpose(features_all[s])
-
         def book(q):
-            out[q] = out[q] + jnp.dot(
-                features_turned[...], slopes_all[s, :, rows(q, columns)], preferred_element_type=f32
+            out[q] = out[q] + lax.dot_general(
+                features_all[s],
+                slopes_all[s, :, rows(q, columns)],
+                (((0,), (0,)), ((), ())),
+                preferred_element_type=f32,
             )
 
         over(books, book)
@@ -499,10 +500,9 @@
             return jnp.sum(jnp.where(picks, line, 0.0), axis=1, keepdims=True)
 
         lane = lane_of(half)
-        facts = jnp.zeros((half, lanes), f32)
-        first_column = (plane * columns).astype(f32)
+        ids = jnp.zeros((half, lanes), jnp.int32)
         for q in range(books):
-            facts = jnp.where(lane == q, column(block[q : q + 1, :]) - first_column, facts)
+            ids = jnp.where(lane == q, column(block[q : q + 1, :]).astype(jnp.int32) - plane * columns, ids)
         document = column(segments_all[b].astype(f32))
 
         def count(p, total):
@@ -510,10 +510,10 @@
             return total + jnp.sum(jnp.where(same, 1.0, 0.0), axis=1, keepdims=True)
 
         size = lax.fori_loop(0, planes, count, jnp.zeros((half, 1), f32))
-        weight = (planes * length) / ((2 * planes) * size)
-        facts = jnp.where(lane == books, weight, facts)
+        weight = jnp.broadcast_to((planes * length) / ((2 * planes) * size), (half, lanes))
         for s in range(rounds):
-            frame_lanes[s, rows(b, sub), :] = facts[s * sub : (s + 1) * sub]
+            target_lanes[s, rows(b, sub), :] = ids[s * sub : (s + 1) * sub]
+            weight_lanes[s, rows(b, sub), :] = weight[s * sub : (s + 1) * sub]
 
     over(planes, unpack)
 
@@ -523,6 +523,22 @@
 
     def between(low, s, high, also=True):
         return jnp.logical_and(jnp.logical_and(s >= low, s < high), also)
+
+    exchange = remote(swap, both_terms.at[rows(role, half)], swap_sem.at[0], swap_sem.at[1], (1 - role, dp, plane))
+
+    def finish_terms():
+        def add_gap(step, total):
+            gap_copy(step, True).wait_recv()
+            return total + gaps_in[lax.rem(plane + planes - step, planes)]
+
+        gap_total = lax.fori_loop(1, planes, add_gap, gaps[plane])
+        student_terms = (
+            blend_ratio * sharpness_divisor * sharpness_divisor * gap_total + (1.0 - blend_ratio) * own_terms[1]
+        )
+        teacher_terms = own_terms[0]
+        swap[...] = jnp.where(role == 0, student_terms, teacher_terms)
+        both_terms[rows(role, half), :] = jnp.where(role == 0, teacher_terms, student_terms)
+        exchange.start()
 
     @pl.when(middle)
     def _():
@@ -534,26 +550,6 @@
         def _():
             compute_slopes(s - 1)
 
-        @pl.when(between(0, s, rounds))
-        def _():
-            teacher_logits(s)
-
-        @pl.when(between(0, s, rounds - 1, middle))
-        def _():
-            forward(0, s + 1)
-
-        @pl.when(between(0, s, rounds))
-        def _():
-            student_logits(s)
-
-        @pl.when(between(0, s, rounds - 1, middle))
-        def _():
-            forward(1, s + 1)
-
-        @pl.when(between(0, s, rounds - 2))
-        def _():
-            owns(s + 2)
-
         @pl.when(s == rounds)
         def _():
             def send_gaps(step, carry):
@@ -562,6 +558,26 @@
 
             lax.fori_loop(1, planes, send_gaps, 0)
 
+        @pl.when(between(0, s, rounds))
+        def _():
+            teacher_logits(s)
+
+        @pl.when(between(0, s, rounds - 1, middle))
+        def _():
+            forward(0, s + 1)
+
+        @pl.when(between(0, s, rounds))
+        def _():
+            student_logits(s)
+
+        @pl.when(between(0, s, rounds - 1, middle))
+        def _():
+            forward(1, s + 1)
+
+        @pl.when(between(0, s, rounds - 2))
+        def _():
+            owns(s + 2)
+
         @pl.when(between(3, s, rounds + 3))
         def _():
             add_gradient(s - 3)
@@ -574,22 +590,12 @@
         def _():
             relay_slopes(s - 1)
 
+        @pl.when(s == rounds)
+        def _():
+            finish_terms()
+
     over(rounds + 3, iteration)
 
-    def add_gap(step, total):
-        gap_copy(step, True).wait_recv()
-        return total + gaps_in[lax.rem(plane + planes - step, planes)]
-
-    gap_total = lax.fori_loop(1, planes, add_gap, gaps[plane])
-    student_terms = (
-        blend_ratio * sharpness_divisor * sharpness_divisor * gap_total + (1.0 - blend_ratio) * own_terms[1]
-    )
-    teacher_terms = own_terms[0]
-    mine = jnp.where(role == 0, teacher_terms, student_terms)
-    swap[...] = jnp.where(role == 0, student_terms, teacher_terms)
-    exchange = remote(swap, both_terms.at[rows(role, half)], swap_sem.at[0], swap_sem.at[1], (1 - role, dp, plane))
-    exchange.start()
-    both_terms[rows(role, half), :] = mine
     exchange.wait()
     terms_out[...] = jnp.transpose(both_terms[...])[2 * pitch : 2 * pitch + books]
 
@@ -675,6 +681,7 @@
             pltpu.VMEM((books, group, columns), f32),
             pltpu.VMEM((planes, books, rows_here), jnp.int32),
             pltpu.VMEM((planes, 1, rows_here), jnp.int32),
+            pltpu.VMEM((rounds, group, lanes), jnp.int32),
             pltpu.VMEM((rounds, group, lanes), f32),
             pltpu.VMEM((2 * group, lanes), f32),
             pltpu.VMEM((rounds, planes, 4 * pitch, 2 * group), f32),
@@ -684,7 +691,6 @@
             pltpu.VMEM((2, half, lanes), f32),
             pltpu.VMEM((half, lanes), f32),
             pltpu.VMEM((rows_here, lanes), f32),
-            pltpu.VMEM((share, places * group), bf16),
             dma((2, 2, rounds, planes)),
             dma((2, rounds, planes)),
             dma((2, rounds)),

time: 117 us -> 115 us (0.983)
  Pallas kernels: 114 us -> 111 us
    pallas_call x1, Pallas kernels: 114 us -> 111 us  [on_device(): pl.pallas_call(functools.partial(kernel, sizes), out_shape=(pltpu.VMEM((b...]
where the time goes in v3:
time: 115 us; the launch traced here: 114 us
  Pallas kernels  111 us (97%)
  local copies, waits for them, and re-layouts  2.42 us (2%)
    pallas_call x1, Pallas kernels, on_device(): pl.pallas_call(functools.partial(kernel, sizes), out_shape=(pltpu.VMEM((b...  111 us
    unnamed x4, local copies, waits for them, and re-layouts  2.42 us

profile of v3, /device:TPU:0, one launch (start us, length us, event | category | flops | bytes accessed | tf_op | source)
XLA Modules:
  0.0 114.1 jit_solution(16345200269782714597)
XLA Ops:
  0.6 111.1 %distill.1 = (f32[4,448,512]{2,1,0:T(8,128)S(1)}, f32[4,128]{1,0:T(4,128)}) custom-call(bf16[128,5120]{1,0:T(8,128)(2,1)} %bitcast.10, bf16[128,3584]{1,0:T(8,128)(2,1)} %bitcast.11, f32[40,128]{1,0:T(8,128)} %bitcast.12, f32[28,128]{1,0:T(8,128)} %bitcast.13, bf16[4,5120,512]{2,1,0:T(8,128)(2,1)} %teacher_weights_in.1, ...), custom_call_target="tpu_custom_call" | custom-call | tf_op jit(solution)/shard_map/distill/pallas_call | solution.py:662
  111.7 0.0 copy-start
  111.7 1.8 %copy.12 = f32[4,448,512]{2,1,0:T(8,128)} copy(f32[4,448,512]{2,1,0:T(8,128)S(1)} %get-tuple-element.6) | data formatting | bytes 7340032
  113.5 0.0 copy-done
  113.6 0.6 copy.13
Async XLA Ops:
  111.7 1.9 %copy-start = (f32[4,128]{1,0:T(4,128)S(1)}, f32[4,128]{1,0:T(4,128)}, u32[]{:S(2)}) copy-start(f32[4,128]{1,0:T(4,128)} %get-tuple-element.5) | copy-start | bytes 6148
